TPU v7x, 512 devices: a whole 4x8x8 slice. The times are simulated.
512 devices in a mesh: gx: 4 (over x_lo, core), gy: 8 (over y), gz: 16 (over x_hi, z).
Axes of the slice: x: 4 (x_hi: 2, x_lo: 2; x = x_hi * 2 + x_lo), y: 8, z: 8, core: 2. Of those that a mesh axis runs over, the one named last changes fastest.
Arguments:
- features: bfloat16 [4, 8, 16, 16, 3200], P('gx', 'gy', 'gz'), may hold values from -6 to 6
- box_atoms: int32 [4, 8, 16], P('gx', 'gy', 'gz'), may hold values from 5 to 16, as said below
- edge_count: int32 [4, 8, 16], P('gx', 'gy', 'gz'), may hold values from 85 to 256, as said below
- edge_tower: int32 [4, 8, 16, 256], P('gx', 'gy', 'gz'), may hold values from 0 to 47, as said below
- edge_plate: int32 [4, 8, 16, 256], P('gx', 'gy', 'gz'), may hold values from 0 to 143, as said below
- wigner: float32 [4, 8, 16, 115, 256], P('gx', 'gy', 'gz'), may hold values from -1 to 1, as said below
- radial: bfloat16 [4, 8, 16, 256, 128], P('gx', 'gy', 'gz'), may hold values from 0.049804688 to 0.5
- so2_zero: bfloat16 [640, 640], replicated, may hold values from -0.25 to 0.25
- so2_one: bfloat16 [2, 512, 512], replicated, may hold values from -0.1875 to 0.1875
- so2_two: bfloat16 [2, 384, 384], replicated, may hold values from -0.21875 to 0.21875
Outputs:
- updated: bfloat16 [4, 8, 16, 16, 3200], P('gx', 'gy', 'gz')
Inputs may be any that keep to these rules, and one draw needn't show every extreme that they name: `box_atoms`: the fullest box holds exactly 16 atoms in every draw; counts span a factor of three. `edge_count`: some device holds exactly 256 live edges in every draw. `edge_tower`: every entry d * 16 + a names an atom a present in tower box d, in live and padded slots alike. `edge_plate`: every entry p * 16 + a names an atom a present in plate box p, in live and padded slots alike. `wigner`: for each edge and degree, the rows are rows of an orthogonal matrix.
All inputs are finite; a program needn't handle non-finite values.
Results may differ from a plain program's by a relative error of at most 0.007.
Values may be sent and summed in bfloat16 or wider, within the bound.
A program may use at most 64 MiB of HBM per device.

v0:
```python
import jax
import jax.numpy as jnp
from jax import lax
from jax.sharding import PartitionSpec as P

DEGREE = 4
ORDER = 2


def from_behind(block, axis, distance):
    devices = range(lax.axis_size(axis))
    route = [((i - distance) % len(devices), i) for i in devices]
    return lax.ppermute(block, axis, route)


def extended(block, sides, width):
    for axis, dim in sides:
        count = lax.axis_size(axis)
        forward = [(i, i + 1) for i in range(count - 1)]
        forward.append((count - 1, 0))
        backward = [(target, source) for source, target in forward]
        low = lax.ppermute(
            lax.slice_in_dim(block, block.shape[dim] - width, None, axis=dim), axis, forward
        )
        high = lax.ppermute(lax.slice_in_dim(block, 0, width, axis=dim), axis, backward)
        block = jnp.concatenate([low, block, high], axis=dim)
    return block


def rotate_forward(edge_rows, wig):
    pieces = {}
    offset = 0
    for degree in range(DEGREE + 1):
        within = min(degree, ORDER)
        for azimuth in range(-within, within + 1):
            summed = jnp.zeros((edge_rows.shape[0], edge_rows.shape[2]), jnp.float32)
            for column in range(-degree, degree + 1):
                summed = (
                    summed
                    + wig[offset][:, None] * edge_rows[:, degree * degree + degree + column, :]
                )
                offset += 1
            pieces[degree, azimuth] = summed
    return pieces


def rotate_back(pieces, wig):
    blocks = []
    offset = 0
    for degree in range(DEGREE + 1):
        within = min(degree, ORDER)
        span_cols = 2 * degree + 1
        summed = [None] * span_cols
        for azimuth in range(-within, within + 1):
            for column in range(span_cols):
                product = wig[offset][:, None] * pieces[degree, azimuth]
                summed[column] = product if summed[column] is None else summed[column] + product
                offset += 1
        blocks.extend(summed)
    return jnp.stack(blocks, axis=1)


def mix_orders(pieces, gate, so2_zero, so2_one, so2_two):
    channels = gate.shape[1]

    def lowered(degree, azimuth):
        return (pieces[degree, azimuth] * gate).astype(jnp.bfloat16)

    result = {}
    zeroth = jnp.concatenate([lowered(degree, 0) for degree in range(DEGREE + 1)], axis=1)
    mixed = jnp.dot(zeroth, so2_zero, preferred_element_type=jnp.float32)
    for degree in range(DEGREE + 1):
        result[degree, 0] = mixed[:, degree * channels : (degree + 1) * channels]
    for azimuth, table in ((1, so2_one), (2, so2_two)):
        degrees = list(range(azimuth, DEGREE + 1))
        plus = jnp.concatenate([lowered(degree, azimuth) for degree in degrees], axis=1)
        minus = jnp.concatenate([lowered(degree, -azimuth) for degree in degrees], axis=1)
        real_part = jnp.dot(plus, table[0], preferred_element_type=jnp.float32) - jnp.dot(
            minus, table[1], preferred_element_type=jnp.float32
        )
        imag_part = jnp.dot(plus, table[1], preferred_element_type=jnp.float32) + jnp.dot(
            minus, table[0], preferred_element_type=jnp.float32
        )
        for place, degree in enumerate(degrees):
            result[degree, azimuth] = real_part[:, place * channels : (place + 1) * channels]
            result[degree, -azimuth] = imag_part[:, place * channels : (place + 1) * channels]
    return result


def edge_message(source_rows, wig, gate, live, so2_zero, so2_one, so2_two):
    channels = gate.shape[1]
    shaped = source_rows.reshape(source_rows.shape[0], -1, channels)
    pieces = rotate_forward(shaped, wig)
    mixed = mix_orders(pieces, gate, so2_zero, so2_one, so2_two)
    message = rotate_back(mixed, wig).reshape(source_rows.shape[0], -1)
    return jnp.where(live[:, None], message, 0.0).astype(jnp.bfloat16)


def tower_return(piece, offset):
    return from_behind(piece.astype(jnp.bfloat16), "gx", offset).astype(piece.dtype)


def plate_return_deep(piece, offset):
    return from_behind(piece.astype(jnp.bfloat16), "gz", offset).astype(piece.dtype)


def plate_return_wide(piece, offset):
    return from_behind(piece.astype(jnp.bfloat16), "gy", offset).astype(piece.dtype)


def body(
    features,
    box_atoms,
    edge_count,
    edge_tower,
    edge_plate,
    wigner,
    radial,
    so2_zero,
    so2_one,
    so2_two,
):
    atoms = features.shape[3]
    feature_width = features.shape[4]
    edges = edge_tower.shape[3]
    tower = extended(features, (("gx", 0),), 1).reshape(3 * atoms, feature_width)
    plate = extended(features, (("gy", 1), ("gz", 2)), 1).reshape(9 * atoms, feature_width)
    tower_index = edge_tower.reshape(edges)
    plate_index = edge_plate.reshape(edges)
    rotation = wigner.reshape(wigner.shape[3], edges)
    gate_rows = radial.reshape(edges, radial.shape[4])
    count_here = edge_count.reshape(())
    dims_first = (((0,), (0,)), ((), ()))
    tower_pick = (
        lax.broadcasted_iota(jnp.int32, (3 * atoms, edges), 0) == tower_index[None, :]
    ).astype(jnp.bfloat16)
    plate_pick = (
        lax.broadcasted_iota(jnp.int32, (9 * atoms, edges), 0) == plate_index[None, :]
    ).astype(jnp.bfloat16)
    source_rows = lax.dot_general(tower_pick, tower, dims_first, preferred_element_type=jnp.float32)
    target_rows = lax.dot_general(plate_pick, plate, dims_first, preferred_element_type=jnp.float32)
    live = jnp.arange(edges, dtype=jnp.int32) < count_here
    block_gate = gate_rows.astype(jnp.float32)
    to_plate = edge_message(source_rows, rotation, block_gate, live, so2_zero, so2_one, so2_two)
    plate_sum = jnp.dot(plate_pick, to_plate, preferred_element_type=jnp.float32)
    to_tower = edge_message(target_rows, rotation, block_gate, live, so2_zero, so2_one, so2_two)
    tower_sum = jnp.dot(tower_pick, to_tower, preferred_element_type=jnp.float32)
    tower_sum, plate_sum = (tower_sum, plate_sum)
    tower_parts = tower_sum.reshape(3, atoms, feature_width)
    gathered = tower_parts[1] + tower_return(tower_parts[0], -1) + tower_return(tower_parts[2], 1)
    plate_parts = plate_sum.reshape(3, 3, atoms, feature_width)
    along_y = (
        plate_parts[1]
        + plate_return_wide(plate_parts[0], -1)
        + plate_return_wide(plate_parts[2], 1)
    )
    plate_total = along_y[1] + plate_return_deep(along_y[0], -1) + plate_return_deep(along_y[2], 1)
    updated = features.reshape(atoms, feature_width).astype(jnp.float32) + (gathered + plate_total)
    present = jnp.arange(atoms, dtype=jnp.int32) < box_atoms.reshape(())
    return jnp.where(present[:, None], updated, 0.0).astype(jnp.bfloat16).reshape(features.shape)


def solution(mesh):
    placed = (
        P("gx", "gy", "gz", None, None),
        P("gx", "gy", "gz"),
        P("gx", "gy", "gz"),
        P("gx", "gy", "gz", None),
        P("gx", "gy", "gz", None),
        P("gx", "gy", "gz", None, None),
        P("gx", "gy", "gz", None, None),
        P(),
        P(),
        P(),
    )
    return jax.shard_map(
        body, mesh=mesh, in_specs=placed, out_specs=P("gx", "gy", "gz", None, None), check_vma=False
    )
```

profile of v0, /device:TPU:24, one launch (start us, length us, event | category | flops | bytes accessed | tf_op | source)
XLA Modules:
  0.0 88.8 jit_solution(15888835899640734459)
XLA Ops:
  0.0 2.0 %collective-permute-start.6 = (bf16[1,1,1,16,3200]{4,3,2,1,0:T(8,128)(2,1)}, bf16[1,1,1,16,3200]{4,3,2,1,0:T(8,128)(2,1)S(1)}, u32[]{:S(2)}, u32[]{:S(2)}) collective-permute-start(bf16[1,1,1,16,3200]{4,3,2,1,0:T(8,128)(2,1)} %param.10), channel_id=1, source_target_pairs={{0,128},{128,256},{256,384},{384,0},{1,129},{129,257},{257,385},{3... | collective-permute-start | bytes 307208 | tf_op jit(solution)/shard_map/ppermute | solution.py:22
  2.1 2.4 %collective-permute-start.1 = (bf16[1,1,1,16,3200]{4,3,2,1,0:T(8,128)(2,1)}, bf16[1,1,1,16,3200]{4,3,2,1,0:T(8,128)(2,1)S(1)}, u32[]{:S(2)}, u32[]{:S(2)}) collective-permute-start(bf16[1,1,1,16,3200]{4,3,2,1,0:T(8,128)(2,1)} %param.10), channel_id=1, source_target_pairs={{16,0},{32,16},{48,32},{64,48},{80,64},{96,80},{112,96},{0,112},{1... | collective-permute-start | bytes 307208 | tf_op jit(solution)/shard_map/ppermute | solution.py:25
  4.4 4.7 %collective-permute-start = (bf16[1,1,1,16,3200]{4,3,2,1,0:T(8,128)(2,1)}, bf16[1,1,1,16,3200]{4,3,2,1,0:T(8,128)(2,1)S(1)}, u32[]{:S(2)}, u32[]{:S(2)}) collective-permute-start(bf16[1,1,1,16,3200]{4,3,2,1,0:T(8,128)(2,1)} %param.10), channel_id=1, source_target_pairs={{0,16},{16,32},{32,48},{48,64},{64,80},{80,96},{96,112},{112,0},{1... | collective-permute-start | bytes 307208 | tf_op jit(solution)/shard_map/ppermute | solution.py:22
  9.1 3.1 %collective-permute-start.7 = (bf16[1,1,1,16,3200]{4,3,2,1,0:T(8,128)(2,1)}, bf16[1,1,1,16,3200]{4,3,2,1,0:T(8,128)(2,1)S(1)}, u32[]{:S(2)}, u32[]{:S(2)}) collective-permute-start(bf16[1,1,1,16,3200]{4,3,2,1,0:T(8,128)(2,1)} %param.10), channel_id=1, source_target_pairs={{128,0},{256,128},{384,256},{0,384},{129,1},{257,129},{385,257},{1... | collective-permute-start | bytes 307208 | tf_op jit(solution)/shard_map/ppermute | solution.py:25
  12.2 0.7 slice.559
  12.9 0.9 fusion.134
  13.8 0.9 fusion.132
  14.6 0.9 fusion.129
  15.5 0.9 fusion.133
  16.4 0.9 fusion.131
  17.2 0.9 fusion.130
  19.4 0.9 %copy.39 = bf16[1,1,1,256,128]{3,4,2,1,0:T(8,128)(2,1)S(1)} copy(bf16[1,1,1,256,128]{4,3,2,1,0:T(8,128)(2,1)} %param.16) | data formatting | bytes 131072 | tf_op args[6]
  20.4 0.9 %constant_dynamic-update-slice_fusion.1 = bf16[1,3,1,16,3200]{4,3,2,1,0:T(8,128)(2,1)S(1)} fusion(bf16[1,3,1,16,3200]{4,3,2,1,0:T(8,128)(2,1)S(1)} %constant_dynamic-update-slice_fusion.2, bf16[1,1,1,16,3200]{4,3,2,1,0:T(8,128)(2,1)} %param.10), kind=kLoop, calls=%fused_computation.216 | loop fusion | bytes 204800
  21.3 13.4 %collective-permute-start.3 = (bf16[1,3,1,16,3200]{4,3,2,1,0:T(8,128)(2,1)S(1)}, bf16[1,3,1,16,3200]{4,3,2,1,0:T(8,128)(2,1)S(1)}, u32[]{:S(2)}, u32[]{:S(2)}) collective-permute-start(bf16[1,3,1,16,3200]{4,3,2,1,0:T(8,128)(2,1)S(1)} %constant_dynamic-update-slice_fusion), channel_id=1, source_target_pairs={{1,0},{2,1},{3,2},{4,3},{5,4},{6,5},{7,6},{8,7},{9,8},{10,9},{11,1... | collective-permute-start | bytes 921608 | tf_op jit(solution)/shard_map/ppermute | solution.py:25
  34.7 1.9 %collective-permute-start.2 = (bf16[1,3,1,16,3200]{4,3,2,1,0:T(8,128)(2,1)S(1)}, bf16[1,3,1,16,3200]{4,3,2,1,0:T(8,128)(2,1)S(1)}, u32[]{:S(2)}, u32[]{:S(2)}) collective-permute-start(bf16[1,3,1,16,3200]{4,3,2,1,0:T(8,128)(2,1)S(1)} %constant_dynamic-update-slice_fusion), channel_id=1, source_target_pairs={{0,1},{1,2},{2,3},{3,4},{4,5},{5,6},{6,7},{7,8},{8,9},{9,10},{10,1... | collective-permute-start | bytes 921608 | tf_op jit(solution)/shard_map/ppermute | solution.py:22
  36.7 0.9 %pad_maximum_fusion.1 = bf16[3,1,1,16,3200]{4,3,2,1,0:T(8,128)(2,1)S(1)} fusion(bf16[1,1,1,16,3200]{4,3,2,1,0:T(8,128)(2,1)S(1)} %collective-permute-done.7, bf16[1,1,1,16,3200]{4,3,2,1,0:T(8,128)(2,1)} %param.10, bf16[1,1,1,16,3200]{4,3,2,1,0:T(8,128)(2,1)S(1)} %collective-permute-done.6), kind=kLoop, calls=%fused_computation.78 | loop fusion | flops 307200 | bytes 614400 | tf_op jit(solution)/shard_map/concatenate | solution.py:26
  37.6 1.3 %fusion.25 = f32[256,25,128]{0,2,1:T(8,128)S(1)} fusion(bf16[6,25,8,128]{3,2,1,0:T(8,128)(2,1)S(1)} %bitcast.1035, s32[256]{0:T(256)} %bitcast.1364), kind=kOutput, calls=%fused_computation.75 | convolution fusion | flops 78655488 | bytes 3585024 | tf_op jit(solution)/shard_map/dot_general | solution.py:140
  39.3 0.8 copy-done.1
  42.0 6.7 %collective-permute-done.2 = bf16[1,3,1,16,3200]{4,3,2,1,0:T(8,128)(2,1)S(1)} collective-permute-done((bf16[1,3,1,16,3200]{4,3,2,1,0:T(8,128)(2,1)S(1)}, bf16[1,3,1,16,3200]{4,3,2,1,0:T(8,128)(2,1)S(1)}, u32[]{:S(2)}, u32[]{:S(2)}) %collective-permute-start.2) | collective-permute-done | bytes 307232 | tf_op jit(solution)/shard_map/ppermute | solution.py:22
  48.9 0.8 fusion.2
  59.7 0.8 fusion.1
  61.1 0.7 fusion.136
  61.8 3.5 %collective-permute-start.9 = (bf16[3,16,3200]{2,1,0:T(8,128)(2,1)S(1)}, bf16[3,16,3200]{2,1,0:T(8,128)(2,1)S(1)}, u32[]{:S(2)}, u32[]{:S(2)}) collective-permute-start(bf16[3,16,3200]{2,1,0:T(8,128)(2,1)S(1)} %bitcast.1037), channel_id=1, source_target_pairs={{112,0},{0,16},{16,32},{32,48},{48,64},{64,80},{80,96},{96,112},{1... | collective-permute-start | bytes 921608 | tf_op jit(solution)/shard_map/ppermute | solution.py:13
  65.3 2.4 %collective-permute-start.8 = (bf16[3,16,3200]{2,1,0:T(8,128)(2,1)S(1)}, bf16[3,16,3200]{2,1,0:T(8,128)(2,1)S(1)}, u32[]{:S(2)}, u32[]{:S(2)}) collective-permute-start(bf16[3,16,3200]{2,1,0:T(8,128)(2,1)S(1)} %bitcast.1036), channel_id=1, source_target_pairs={{16,0},{32,16},{48,32},{64,48},{80,64},{96,80},{112,96},{0,112},{1... | collective-permute-start | bytes 921608 | tf_op jit(solution)/shard_map/ppermute | solution.py:13
  67.7 1.9 %collective-permute-start.4 = (bf16[16,3200]{1,0:T(8,128)(2,1)S(1)}, bf16[16,3200]{1,0:T(8,128)(2,1)S(1)}, u32[]{:S(2)}, u32[]{:S(2)}) collective-permute-start(bf16[16,3200]{1,0:T(8,128)(2,1)S(1)} %get-tuple-element.17), channel_id=1, source_target_pairs={{128,0},{256,128},{384,256},{0,384},{129,1},{257,129},{385,257},{1... | collective-permute-start | bytes 307208 | tf_op jit(solution)/shard_map/ppermute | solution.py:13
  69.7 2.4 %collective-permute-start.5 = (bf16[16,3200]{1,0:T(8,128)(2,1)S(1)}, bf16[16,3200]{1,0:T(8,128)(2,1)S(1)}, u32[]{:S(2)}, u32[]{:S(2)}) collective-permute-start(bf16[16,3200]{1,0:T(8,128)(2,1)S(1)} %get-tuple-element.18), channel_id=1, source_target_pairs={{384,0},{0,128},{128,256},{256,384},{385,1},{1,129},{129,257},{257... | collective-permute-start | bytes 307208 | tf_op jit(solution)/shard_map/ppermute | solution.py:13
  72.1 3.6 %collective-permute-done.8 = bf16[3,16,3200]{2,1,0:T(8,128)(2,1)S(1)} collective-permute-done((bf16[3,16,3200]{2,1,0:T(8,128)(2,1)S(1)}, bf16[3,16,3200]{2,1,0:T(8,128)(2,1)S(1)}, u32[]{:S(2)}, u32[]{:S(2)}) %collective-permute-start.8) | collective-permute-done | bytes 307232 | tf_op jit(solution)/shard_map/ppermute | solution.py:13
  75.9 1.9 %collective-permute-start.10 = (bf16[16,3200]{1,0:T(8,128)(2,1)S(1)}, bf16[16,3200]{1,0:T(8,128)(2,1)S(1)}, u32[]{:S(2)}, u32[]{:S(2)}) collective-permute-start(bf16[16,3200]{1,0:T(8,128)(2,1)S(1)} %get-tuple-element.19), channel_id=1, source_target_pairs={{1,0},{2,1},{3,2},{4,3},{5,4},{6,5},{7,6},{8,7},{9,8},{10,9},{11,1... | collective-permute-start | bytes 307208 | tf_op jit(solution)/shard_map/ppermute | solution.py:13
  77.8 3.9 %collective-permute-start.11 = (bf16[16,3200]{1,0:T(8,128)(2,1)S(1)}, bf16[16,3200]{1,0:T(8,128)(2,1)S(1)}, u32[]{:S(2)}, u32[]{:S(2)}) collective-permute-start(bf16[16,3200]{1,0:T(8,128)(2,1)S(1)} %get-tuple-element.20), channel_id=1, source_target_pairs={{15,0},{0,1},{1,2},{2,3},{3,4},{4,5},{5,6},{6,7},{7,8},{8,9},{9,10... | collective-permute-start | bytes 307208 | tf_op jit(solution)/shard_map/ppermute | solution.py:13
  81.8 0.7 collective-permute-done.10
  82.5 5.5 %collective-permute-done.11 = bf16[16,3200]{1,0:T(8,128)(2,1)S(1)} collective-permute-done((bf16[16,3200]{1,0:T(8,128)(2,1)S(1)}, bf16[16,3200]{1,0:T(8,128)(2,1)S(1)}, u32[]{:S(2)}, u32[]{:S(2)}) %collective-permute-start.11) | collective-permute-done | bytes 102432 | tf_op jit(solution)/shard_map/ppermute | solution.py:13
  88.0 0.7 fusion.102
  (102 shorter events, 12.9 us)
Async XLA Ops:
  0.0 56.0 %copy-start = (bf16[640,640]{1,0:T(8,128)(2,1)S(1)}, bf16[640,640]{1,0:T(8,128)(2,1)}, u32[]{:S(2)}) copy-start(bf16[640,640]{1,0:T(8,128)(2,1)} %param.17) | copy-start | bytes 2457604
  0.0 36.7 %collective-permute-start.6 = (bf16[1,1,1,16,3200]{4,3,2,1,0:T(8,128)(2,1)}, bf16[1,1,1,16,3200]{4,3,2,1,0:T(8,128)(2,1)S(1)}, u32[]{:S(2)}, u32[]{:S(2)}) collective-permute-start(bf16[1,1,1,16,3200]{4,3,2,1,0:T(8,128)(2,1)} %param.10), channel_id=1, source_target_pairs={{0,128},{128,256},{256,384},{384,0},{1,129},{129,257},{257,385},{3... | collective-permute-start | bytes 307208 | tf_op jit(solution)/shard_map/ppermute | solution.py:22
  2.1 19.3 %collective-permute-start.1 = (bf16[1,1,1,16,3200]{4,3,2,1,0:T(8,128)(2,1)}, bf16[1,1,1,16,3200]{4,3,2,1,0:T(8,128)(2,1)S(1)}, u32[]{:S(2)}, u32[]{:S(2)}) collective-permute-start(bf16[1,1,1,16,3200]{4,3,2,1,0:T(8,128)(2,1)} %param.10), channel_id=1, source_target_pairs={{16,0},{32,16},{48,32},{64,48},{80,64},{96,80},{112,96},{0,112},{1... | collective-permute-start | bytes 307208 | tf_op jit(solution)/shard_map/ppermute | solution.py:25
  4.4 15.9 %collective-permute-start = (bf16[1,1,1,16,3200]{4,3,2,1,0:T(8,128)(2,1)}, bf16[1,1,1,16,3200]{4,3,2,1,0:T(8,128)(2,1)S(1)}, u32[]{:S(2)}, u32[]{:S(2)}) collective-permute-start(bf16[1,1,1,16,3200]{4,3,2,1,0:T(8,128)(2,1)} %param.10), channel_id=1, source_target_pairs={{0,16},{16,32},{32,48},{48,64},{64,80},{80,96},{96,112},{112,0},{1... | collective-permute-start | bytes 307208 | tf_op jit(solution)/shard_map/ppermute | solution.py:22
  9.1 27.6 %collective-permute-start.7 = (bf16[1,1,1,16,3200]{4,3,2,1,0:T(8,128)(2,1)}, bf16[1,1,1,16,3200]{4,3,2,1,0:T(8,128)(2,1)S(1)}, u32[]{:S(2)}, u32[]{:S(2)}) collective-permute-start(bf16[1,1,1,16,3200]{4,3,2,1,0:T(8,128)(2,1)} %param.10), channel_id=1, source_target_pairs={{128,0},{256,128},{384,256},{0,384},{129,1},{257,129},{385,257},{1... | collective-permute-start | bytes 307208 | tf_op jit(solution)/shard_map/ppermute | solution.py:25
  21.3 20.7 %collective-permute-start.3 = (bf16[1,3,1,16,3200]{4,3,2,1,0:T(8,128)(2,1)S(1)}, bf16[1,3,1,16,3200]{4,3,2,1,0:T(8,128)(2,1)S(1)}, u32[]{:S(2)}, u32[]{:S(2)}) collective-permute-start(bf16[1,3,1,16,3200]{4,3,2,1,0:T(8,128)(2,1)S(1)} %constant_dynamic-update-slice_fusion), channel_id=1, source_target_pairs={{1,0},{2,1},{3,2},{4,3},{5,4},{6,5},{7,6},{8,7},{9,8},{10,9},{11,1... | collective-permute-start | bytes 921608 | tf_op jit(solution)/shard_map/ppermute | solution.py:25
  34.7 14.0 %collective-permute-start.2 = (bf16[1,3,1,16,3200]{4,3,2,1,0:T(8,128)(2,1)S(1)}, bf16[1,3,1,16,3200]{4,3,2,1,0:T(8,128)(2,1)S(1)}, u32[]{:S(2)}, u32[]{:S(2)}) collective-permute-start(bf16[1,3,1,16,3200]{4,3,2,1,0:T(8,128)(2,1)S(1)} %constant_dynamic-update-slice_fusion), channel_id=1, source_target_pairs={{0,1},{1,2},{2,3},{3,4},{4,5},{5,6},{6,7},{7,8},{8,9},{9,10},{10,1... | collective-permute-start | bytes 921608 | tf_op jit(solution)/shard_map/ppermute | solution.py:22
  39.0 1.1 %copy-start.1 = (bf16[2,384,384]{2,1,0:T(8,128)(2,1)S(1)}, bf16[2,384,384]{2,1,0:T(8,128)(2,1)}, u32[]{:S(2)}) copy-start(bf16[2,384,384]{2,1,0:T(8,128)(2,1)} %param.19) | copy-start | bytes 1769476
  41.7 7.2 %copy-start.4 = (s32[1,1,1,256]{3,2,1,0:T(1,128)S(1)}, s32[1,1,1,256]{3,2,1,0:T(1,128)}, u32[]{:S(2)}) copy-start(s32[1,1,1,256]{3,2,1,0:T(1,128)} %param.14) | copy-start | bytes 3076
  50.6 1.2 %copy-start.5 = (bf16[2,512,512]{2,1,0:T(8,128)(2,1)S(1)}, bf16[2,512,512]{2,1,0:T(8,128)(2,1)}, u32[]{:S(2)}) copy-start(bf16[2,512,512]{2,1,0:T(8,128)(2,1)} %param.18) | copy-start | bytes 3145732
  59.7 0.8 copy-start.3
  61.8 10.3 %collective-permute-start.9 = (bf16[3,16,3200]{2,1,0:T(8,128)(2,1)S(1)}, bf16[3,16,3200]{2,1,0:T(8,128)(2,1)S(1)}, u32[]{:S(2)}, u32[]{:S(2)}) collective-permute-start(bf16[3,16,3200]{2,1,0:T(8,128)(2,1)S(1)} %bitcast.1037), channel_id=1, source_target_pairs={{112,0},{0,16},{16,32},{32,48},{48,64},{64,80},{80,96},{96,112},{1... | collective-permute-start | bytes 921608 | tf_op jit(solution)/shard_map/ppermute | solution.py:13
  65.3 10.4 %collective-permute-start.8 = (bf16[3,16,3200]{2,1,0:T(8,128)(2,1)S(1)}, bf16[3,16,3200]{2,1,0:T(8,128)(2,1)S(1)}, u32[]{:S(2)}, u32[]{:S(2)}) collective-permute-start(bf16[3,16,3200]{2,1,0:T(8,128)(2,1)S(1)} %bitcast.1036), channel_id=1, source_target_pairs={{16,0},{32,16},{48,32},{64,48},{80,64},{96,80},{112,96},{0,112},{1... | collective-permute-start | bytes 921608 | tf_op jit(solution)/shard_map/ppermute | solution.py:13
  67.7 14.1 %collective-permute-start.4 = (bf16[16,3200]{1,0:T(8,128)(2,1)S(1)}, bf16[16,3200]{1,0:T(8,128)(2,1)S(1)}, u32[]{:S(2)}, u32[]{:S(2)}) collective-permute-start(bf16[16,3200]{1,0:T(8,128)(2,1)S(1)} %get-tuple-element.17), channel_id=1, source_target_pairs={{128,0},{256,128},{384,256},{0,384},{129,1},{257,129},{385,257},{1... | collective-permute-start | bytes 307208 | tf_op jit(solution)/shard_map/ppermute | solution.py:13
  69.7 12.2 %collective-permute-start.5 = (bf16[16,3200]{1,0:T(8,128)(2,1)S(1)}, bf16[16,3200]{1,0:T(8,128)(2,1)S(1)}, u32[]{:S(2)}, u32[]{:S(2)}) collective-permute-start(bf16[16,3200]{1,0:T(8,128)(2,1)S(1)} %get-tuple-element.18), channel_id=1, source_target_pairs={{384,0},{0,128},{128,256},{256,384},{385,1},{1,129},{129,257},{257... | collective-permute-start | bytes 307208 | tf_op jit(solution)/shard_map/ppermute | solution.py:13
  72.1 16.0 %copy-start.2 = (bf16[1,1,1,16,3200]{4,3,2,1,0:T(8,128)(2,1)S(1)}, bf16[1,1,1,16,3200]{4,3,2,1,0:T(8,128)(2,1)}, u32[]{:S(2)}) copy-start(bf16[1,1,1,16,3200]{4,3,2,1,0:T(8,128)(2,1)} %param.10) | copy-start | bytes 307204
  75.9 6.6 %collective-permute-start.10 = (bf16[16,3200]{1,0:T(8,128)(2,1)S(1)}, bf16[16,3200]{1,0:T(8,128)(2,1)S(1)}, u32[]{:S(2)}, u32[]{:S(2)}) collective-permute-start(bf16[16,3200]{1,0:T(8,128)(2,1)S(1)} %get-tuple-element.19), channel_id=1, source_target_pairs={{1,0},{2,1},{3,2},{4,3},{5,4},{6,5},{7,6},{8,7},{9,8},{10,9},{11,1... | collective-permute-start | bytes 307208 | tf_op jit(solution)/shard_map/ppermute | solution.py:13
  77.8 10.2 %collective-permute-start.11 = (bf16[16,3200]{1,0:T(8,128)(2,1)S(1)}, bf16[16,3200]{1,0:T(8,128)(2,1)S(1)}, u32[]{:S(2)}, u32[]{:S(2)}) collective-permute-start(bf16[16,3200]{1,0:T(8,128)(2,1)S(1)} %get-tuple-element.20), channel_id=1, source_target_pairs={{15,0},{0,1},{1,2},{2,3},{3,4},{4,5},{5,6},{6,7},{7,8},{8,9},{9,10... | collective-permute-start | bytes 307208 | tf_op jit(solution)/shard_map/ppermute | solution.py:13
where the time goes:
time: 89.6 us; the launch traced here: 88.8 us
  starting transfers between devices  43.5 us (49%)
  waiting for transfers between devices  16.6 us (19%)
  matrix products  9.61 us (11%)
  local copies, waits for them, and re-layouts  9.13 us (10%)
  other arithmetic  7.89 us (9%)
  between operations  2.02 us (2%)
    ppermute x3, starting transfers between devices, extended(): lax.ppermute(lax.slice_in_dim(block, 0, width, axis=dim), axis, backward)  18.9 us
    ppermute x6, starting transfers between devices, from_behind(): return lax.ppermute(block, axis, route)  16 us
    ppermute x6, waiting for transfers between devices, from_behind(): return lax.ppermute(block, axis, route)  9.85 us
    ppermute x3, starting transfers between devices, extended(): lax.ppermute(lax.slice_in_dim(block, block.shape[dim] - width, None, axis...  8.66 us
    ppermute x3, waiting for transfers between devices, extended(): lax.ppermute(lax.slice_in_dim(block, block.shape[dim] - width, None, axis...  6.72 us
    slice x4, local copies, waits for them, and re-layouts, rotate_forward(): wig[offset][:, None] * edge_rows[:, degree * degree + degree + column, :]  3.46 us
    unnamed x15, local copies, waits for them, and re-layouts  3.12 us
    unnamed x29, other arithmetic  2.79 us
  transfers between devices with their start and end apart: 12, of which 4 were waited for; matrix products, arithmetic and copies ran while one was open for 14% of the time, Pallas kernels for 0%

commit v1 on v0

v1 whole, which is shorter than its diff:
```python
import jax
import jax.numpy as jnp
from jax import lax
from jax.experimental import pallas as pl
from jax.experimental.pallas import tpu as pltpu
from jax.sharding import PartitionSpec as P

MESH = pl.DeviceIdType.MESH
DEGREE = 4
ORDER = 2
C = 128
A = 16
COEFS = 25
F = COEFS * C
F32 = jnp.float32
BF16 = jnp.bfloat16
NT = (((1,), (1,)), ((), ()))
TN = (((0,), (0,)), ((), ()))

WIG = {}
_at = 0
for _l in range(DEGREE + 1):
    for _m in range(-min(_l, ORDER), min(_l, ORDER) + 1):
        WIG[_l, _m] = _at
        _at += 2 * _l + 1
ROWS = _at

CHUNKS = (((4,), 16, 9), ((3,), 9, 7), ((0, 1, 2), 0, 9))
NCH = len(CHUNKS)
OWN = 4
XLOW, XHIGH = 9, 10


def kernel(
    feat_h, atoms_h, count_h, et_h, ep_h, wig_h, rad_h, w0_h, w1_h, w2_h,
    out,
    x, et, ep, wig, rad, w0, w1, w2, wb, gate, w0t, w1t, w2t, pick_t, pick_p,
    g, l0, l1, l2, y0, y1, y2, msg,
    sp, sc, ry, sz, rz, acc, st, tc, rt,
    atoms_s, count_s, local, fs, fr, bs, br,
):
    gx, gy, gz = lax.axis_index("gx"), lax.axis_index("gy"), lax.axis_index("gz")
    nx, ny, nz = lax.axis_size("gx"), lax.axis_size("gy"), lax.axis_size("gz")
    up = {"gx": lax.rem(gx + 1, nx), "gy": lax.rem(gy + 1, ny), "gz": lax.rem(gz + 1, nz)}
    down = {
        "gx": lax.rem(gx + nx - 1, nx),
        "gy": lax.rem(gy + ny - 1, ny),
        "gz": lax.rem(gz + nz - 1, nz),
    }

    def remote(src, dst, send, recv, axis, where):
        return pltpu.make_async_remote_copy(
            src_ref=src, dst_ref=dst, send_sem=send, recv_sem=recv,
            device_id={axis: where[axis]}, device_id_type=MESH,
        )

    loads = [
        pltpu.make_async_copy(src, dst, local.at[i])
        for i, (src, dst) in enumerate(
            (
                (feat_h, x.at[OWN]), (wig_h, wig), (et_h, et), (ep_h, ep), (rad_h, rad),
                (w0_h, w0), (w1_h, w1), (w2_h, w2), (atoms_h, atoms_s), (count_h, count_s),
            )
        )
    ]
    barrier = pltpu.get_barrier_semaphore()
    for axis in ("gx", "gy", "gz"):
        for where in (up, down):
            pl.semaphore_signal(
                barrier, inc=1, device_id={axis: where[axis]}, device_id_type=MESH
            )
    for load in loads:
        load.start()
    loads[0].wait()
    pl.semaphore_wait(barrier, 6)

    def forward(k, src, dst, axis, where):
        return remote(x.at[src], x.at[dst], fs.at[k], fr.at[k], axis, where)

    first = [
        forward(0, OWN, 3, "gz", up), forward(1, OWN, 5, "gz", down),
        forward(2, OWN, 1, "gy", up), forward(3, OWN, 7, "gy", down),
        forward(4, OWN, XLOW, "gx", up), forward(5, OWN, XHIGH, "gx", down),
    ]
    relays = [
        forward(6, 3, 0, "gy", up), forward(7, 3, 6, "gy", down),
        forward(8, 5, 2, "gy", up), forward(9, 5, 8, "gy", down),
    ]
    for copy in first:
        copy.start()

    for load in loads[1:]:
        load.wait()
    for o in range(ROWS):
        wb[o] = jnp.broadcast_to(wig[o], (8, wig.shape[2]))
    gate[...] = rad[...].T.astype(F32)
    live = lax.broadcasted_iota(jnp.int32, et.shape, 1) < count_s[0, 0]
    edges = et.shape[1]
    here_t = jnp.where(live, et[...], -1)
    here_p = jnp.where(live, ep[...], -1)
    pick_t[...] = (
        lax.broadcasted_iota(jnp.int32, (3 * A, edges), 0) == here_t
    ).astype(F32).astype(BF16)
    pick_p[...] = (
        lax.broadcasted_iota(jnp.int32, (9 * A, edges), 0) == here_p
    ).astype(F32).astype(BF16)

    def column(i):
        return pl.ds(pl.multiple_of(i * C, C), C)

    def turn0(i, c):
        w0t[column(i), :] = w0[:, column(i)].T
        return c

    def turn1(i, c):
        w1t[column(i), 0:512] = w1[1, :, column(i)].T
        w1t[column(i), 512:1024] = w1[0, :, column(i)].T
        return c

    def turn2(i, c):
        w2t[column(i), 0:384] = w2[1, :, column(i)].T
        w2t[column(i), 384:768] = w2[0, :, column(i)].T
        return c

    lax.fori_loop(0, 5, turn0, 0)
    lax.fori_loop(0, 4, turn1, 0)
    lax.fori_loop(0, 3, turn2, 0)

    def spread(o):
        row = wb[o]
        return jnp.concatenate([row, row], axis=0)

    def gather_tower(i, c):
        col = column(i)
        block = jnp.concatenate([x[XLOW, :, col], x[OWN, :, col], x[XHIGH, :, col]], axis=0)
        g[i] = lax.dot_general(block, pick_t[...], TN, preferred_element_type=F32)
        return c

    def gather_plate(i, c):
        block = x[0:9, :, column(i)].reshape(9 * A, C)
        g[i] = lax.dot_general(block, pick_p[...], TN, preferred_element_type=F32)
        return c

    def rotate(t, c):
        base = pl.multiple_of(t * 16, 16)
        tile = pl.ds(base, 16)
        scale = gate[tile, :]
        for l in range(DEGREE + 1):
            xs = [g[l * l + j, tile, :] for j in range(2 * l + 1)]
            for m in range(-min(l, ORDER), min(l, ORDER) + 1):
                total = spread(WIG[l, m]) * xs[0]
                for j in range(1, 2 * l + 1):
                    total = total + spread(WIG[l, m] + j) * xs[j]
                low = (total * scale).astype(BF16)
                if m == 0:
                    l0[pl.ds(base + l * C, 16), :] = low
                else:
                    ref, size = (l1, 4 * C) if abs(m) == 1 else (l2, 3 * C)
                    at = base + (l - abs(m)) * C
                    if m > 0:
                        ref[pl.ds(at + size, 16), :] = low
                    else:
                        ref[pl.ds(at, 16), :] = -low
                        ref[pl.ds(at + 2 * size, 16), :] = low
        return c

    def mix():
        y0[...] = jnp.dot(w0t[...], l0[...], preferred_element_type=F32)
        y1[0] = jnp.dot(w1t[...], l1[0:1024, :], preferred_element_type=F32)
        y1[1] = jnp.dot(w1t[...], l1[512:1536, :], preferred_element_type=F32)
        y2[0] = jnp.dot(w2t[...], l2[0:768, :], preferred_element_type=F32)
        y2[1] = jnp.dot(w2t[...], l2[384:1152, :], preferred_element_type=F32)

    def rotate_back(degrees):
        def step(t, c):
            base = pl.multiple_of(t * 16, 16)
            for l in degrees:
                within = min(l, ORDER)
                ys = {}
                for m in range(-within, within + 1):
                    if m == 0:
                        ys[m] = y0[pl.ds(base + l * C, 16), :]
                    else:
                        ref = y1 if abs(m) == 1 else y2
                        ys[m] = ref[0 if m > 0 else 1, pl.ds(base + (l - abs(m)) * C, 16), :]
                for j in range(2 * l + 1):
                    total = None
                    for m in range(-within, within + 1):
                        term = spread(WIG[l, m] + j) * ys[m]
                        total = term if total is None else total + term
                    msg[l * l + j, pl.ds(base, 16), :] = total.astype(BF16)
            return c

        lax.fori_loop(0, 8, step, 0)

    def chunk_cols(q):
        return pl.ds(CHUNKS[q][1] * C, CHUNKS[q][2] * C)

    def back(q, part, axis, where):
        cols = chunk_cols(q)
        side = 0 if where is down else 1
        k = q * 6 + part * 2 + side
        src, dst = ((sp, ry), (sz, rz), (st, rt))[part]
        index = (side, slice(None), slice(None), cols) if part == 0 else (side, slice(None), cols)
        return remote(src.at[index], dst.at[index], bs.at[k], br.at[k], axis, where)

    backs = [
        [[back(q, part, axis, where) for where in (down, up)]
         for part, axis in enumerate(("gy", "gz", "gx"))]
        for q in range(NCH)
    ]

    def along(q):
        cols = chunk_cols(q)
        for copy in backs[q][0]:
            copy.wait_recv()
        for f in (0, 2):
            total = sc[f, :, cols] + ry[0, f, :, cols].astype(F32) + ry[1, f, :, cols].astype(F32)
            sz[f // 2, :, cols] = total.astype(BF16)
        for copy in backs[q][1]:
            copy.start()
        acc[:, cols] = sc[1, :, cols] + ry[0, 1, :, cols].astype(F32) + ry[1, 1, :, cols].astype(F32)

    first[0].wait_recv()
    relays[0].start()
    relays[1].start()
    first[1].wait_recv()
    relays[2].start()
    relays[3].start()

    first[4].wait_recv()
    first[5].wait_recv()
    lax.fori_loop(0, COEFS, gather_tower, 0, unroll=5)
    lax.fori_loop(0, 8, rotate, 0)
    mix()
    for q, (degrees, low, many) in enumerate(CHUNKS):
        rotate_back(degrees)

        def scatter_plate(i, c):
            s = lax.dot_general(pick_p[...], msg[i], NT, preferred_element_type=F32)
            col = column(i)
            for f in range(3):
                sp[0, f, :, col] = s[f * A : (f + 1) * A].astype(BF16)
                sc[f, :, col] = s[(3 + f) * A : (4 + f) * A]
                sp[1, f, :, col] = s[(6 + f) * A : (7 + f) * A].astype(BF16)
            return c

        lax.fori_loop(low, low + many, scatter_plate, 0)
        for copy in backs[q][0]:
            copy.start()

    for copy in first[2:4] + relays:
        copy.wait_recv()
    lax.fori_loop(0, COEFS, gather_plate, 0, unroll=5)
    lax.fori_loop(0, 8, rotate, 0)
    along(0)
    mix()
    along(1)
    along(2)
    for q, (degrees, low, many) in enumerate(CHUNKS):
        rotate_back(degrees)

        def scatter_tower(i, c):
            s = lax.dot_general(pick_t[...], msg[i], NT, preferred_element_type=F32)
            col = column(i)
            st[0, :, col] = s[0:A].astype(BF16)
            tc[:, col] = s[A : 2 * A]
            st[1, :, col] = s[2 * A : 3 * A].astype(BF16)
            return c

        lax.fori_loop(low, low + many, scatter_tower, 0)
        for copy in backs[q][2]:
            copy.start()

    present = lax.broadcasted_iota(jnp.int32, (A, C), 0) < atoms_s[0, 0]
    for q, (degrees, low, many) in enumerate(CHUNKS):
        for copy in backs[q][1] + backs[q][2]:
            copy.wait_recv()

        def finish(i, c):
            col = column(i)
            total = (
                tc[:, col] + rt[0, :, col].astype(F32) + rt[1, :, col].astype(F32)
                + acc[:, col] + rz[0, :, col].astype(F32) + rz[1, :, col].astype(F32)
                + x[OWN, :, col].astype(F32)
            )
            out[:, col] = jnp.where(present, total, 0.0).astype(BF16)
            return c

        lax.fori_loop(low, low + many, finish, 0)
    for copy in first + relays:
        copy.wait_send()
    for q in range(NCH):
        for part in backs[q]:
            for copy in part:
                copy.wait_send()


def body(features, box_atoms, edge_count, edge_tower, edge_plate, wigner, radial, so2_zero, so2_one, so2_two):
    E = edge_tower.shape[3]
    hbm = pl.BlockSpec(memory_space=pl.ANY)
    V = pltpu.VMEM
    dma = pltpu.SemaphoreType.DMA
    result = pl.pallas_call(
        kernel,
        out_shape=jax.ShapeDtypeStruct((A, F), BF16),
        in_specs=[hbm] * 10,
        out_specs=pl.BlockSpec(memory_space=pltpu.VMEM),
        scratch_shapes=[
            V((11, A, F), BF16), V((1, E), jnp.int32), V((1, E), jnp.int32), V((ROWS, 1, E), F32),
            V((E, C), BF16), V((640, 640), BF16), V((2, 512, 512), BF16), V((2, 384, 384), BF16),
            V((ROWS, 8, E), F32), V((C, E), F32),
            V((640, 640), BF16), V((512, 1024), BF16), V((384, 768), BF16),
            V((3 * A, E), BF16), V((9 * A, E), BF16),
            V((COEFS, C, E), F32), V((640, E), BF16), V((1536, E), BF16), V((1152, E), BF16),
            V((640, E), F32), V((2, 512, E), F32), V((2, 384, E), F32), V((COEFS, C, E), BF16),
            V((2, 3, A, F), BF16), V((3, A, F), F32), V((2, 3, A, F), BF16),
            V((2, A, F), BF16), V((2, A, F), BF16), V((A, F), F32),
            V((2, A, F), BF16), V((A, F), F32), V((2, A, F), BF16),
            pltpu.SMEM((1, 1), jnp.int32), pltpu.SMEM((1, 1), jnp.int32), dma((10,)), dma((10,)), dma((10,)), dma((6 * NCH,)), dma((6 * NCH,)),
        ],
        compiler_params=pltpu.CompilerParams(collective_id=0, has_side_effects=True),
        name="layer",
    )(
        features.reshape(A, F), box_atoms.reshape(1, 1), edge_count.reshape(1, 1),
        edge_tower.reshape(1, E), edge_plate.reshape(1, E),
        wigner.reshape(ROWS, 1, E), radial.reshape(E, C), so2_zero, so2_one, so2_two,
    )
    return result.reshape(features.shape)


def solution(mesh):
    boxes = ("gx", "gy", "gz")
    placed = (
        P(*boxes, None, None), P(*boxes), P(*boxes), P(*boxes, None), P(*boxes, None),
        P(*boxes, None, None), P(*boxes, None, None), P(), P(), P(),
    )
    return jax.shard_map(
        body, mesh=mesh, in_specs=placed, out_specs=P(*boxes, None, None), check_vma=False
    )
```

time: 89.6 us -> 47.2 us (0.53)
  the two profiles are of different devices: /device:TPU:24 before, /device:TPU:1 now
where the time goes in v1:
time: 47.2 us; the launch traced here: 47 us
  Pallas kernels  44.2 us (94%)
  local copies, waits for them, and re-layouts  1.54 us (3%)
  between operations  1.3 us (3%)
    pallas_call x1, Pallas kernels, body(): pl.pallas_call(kernel, out_shape=jax.ShapeDtypeStruct((A, F), BF16), in_s...  44.2 us
    unnamed x1, local copies, waits for them, and re-layouts  1.54 us

profile of v1, /device:TPU:1, one launch (start us, length us, event | category | flops | bytes accessed | tf_op | source)
XLA Modules:
  0.0 47.0 jit_solution(15700065250745235667)
XLA Ops:
  1.3 44.2 %layer.1 = bf16[16,3200]{1,0:T(8,128)(2,1)} custom-call(bf16[16,3200]{1,0:T(8,128)(2,1)} %bitcast.12, s32[1,1]{1,0:T(1,128)} %bitcast.8.atoms_h, s32[1,1]{1,0:T(1,128)} %bitcast.9.count_h, s32[1,256]{1,0:T(1,128)} %bitcast.14, s32[1,256]{1,0:T(1,128)} %bitcast.15, f32[115,1,256]{2,1,0:T(1,128)} %bitcast.11, bf16[256,128]{1,0:T(8,128)(2,1)} %bitcast.13, ...), custom_call_target="tpu_custom_call" | custom-call | tf_op jit(solution)/shard_map/layer/pallas_call | solution.py:304
  45.5 1.5 %copy.14 = bf16[1,1,1,16,3200]{4,3,2,1,0:T(8,128)(2,1)} copy(bf16[1,1,1,16,3200]{4,3,2,1,0:T(8,128)(2,1)} %bitcast.10) | data formatting | bytes 204800

commit v2 on v1

--- a/solution.py
+++ b/solution.py
@@ -36,9 +36,10 @@
     out,
     x, et, ep, wig, rad, w0, w1, w2, wb, gate, w0t, w1t, w2t, pick_t, pick_p,
     g, l0, l1, l2, y0, y1, y2, msg,
-    sp, sc, ry, sz, rz, acc, st, tc, rt,
+    sp, sc, ry, sz, rz, st, tc, rt,
     atoms_s, count_s, local, fs, fr, bs, br,
 ):
+    E = et.shape[1]
     gx, gy, gz = lax.axis_index("gx"), lax.axis_index("gy"), lax.axis_index("gz")
     nx, ny, nz = lax.axis_size("gx"), lax.axis_size("gy"), lax.axis_size("gz")
     up = {"gx": lax.rem(gx + 1, nx), "gy": lax.rem(gy + 1, ny), "gz": lax.rem(gz + 1, nz)}
@@ -83,8 +84,8 @@
         forward(4, OWN, XLOW, "gx", up), forward(5, OWN, XHIGH, "gx", down),
     ]
     relays = [
-        forward(6, 3, 0, "gy", up), forward(7, 3, 6, "gy", down),
-        forward(8, 5, 2, "gy", up), forward(9, 5, 8, "gy", down),
+        forward(6, 3, 0, "gy", up), forward(7, 5, 8, "gy", down),
+        forward(8, 7, 6, "gz", up), forward(9, 1, 2, "gz", down),
     ]
     for copy in first:
         copy.start()
@@ -158,18 +159,17 @@
                     ref, size = (l1, 4 * C) if abs(m) == 1 else (l2, 3 * C)
                     at = base + (l - abs(m)) * C
                     if m > 0:
-                        ref[pl.ds(at + size, 16), :] = low
+                        ref[pl.ds(at + size, 16), 0:E] = low
+                        ref[pl.ds(at, 16), E : 2 * E] = low
                     else:
-                        ref[pl.ds(at, 16), :] = -low
-                        ref[pl.ds(at + 2 * size, 16), :] = low
+                        ref[pl.ds(at, 16), 0:E] = -low
+                        ref[pl.ds(at + size, 16), E : 2 * E] = low
         return c
 
     def mix():
         y0[...] = jnp.dot(w0t[...], l0[...], preferred_element_type=F32)
-        y1[0] = jnp.dot(w1t[...], l1[0:1024, :], preferred_element_type=F32)
-        y1[1] = jnp.dot(w1t[...], l1[512:1536, :], preferred_element_type=F32)
-        y2[0] = jnp.dot(w2t[...], l2[0:768, :], preferred_element_type=F32)
-        y2[1] = jnp.dot(w2t[...], l2[384:1152, :], preferred_element_type=F32)
+        y1[...] = jnp.dot(w1t[...], l1[...], preferred_element_type=F32)
+        y2[...] = jnp.dot(w2t[...], l2[...], preferred_element_type=F32)
 
     def rotate_back(degrees):
         def step(t, c):
@@ -182,7 +182,8 @@
                         ys[m] = y0[pl.ds(base + l * C, 16), :]
                     else:
                         ref = y1 if abs(m) == 1 else y2
-                        ys[m] = ref[0 if m > 0 else 1, pl.ds(base + (l - abs(m)) * C, 16), :]
+                        lanes = slice(0, E) if m > 0 else slice(E, 2 * E)
+                        ys[m] = ref[pl.ds(base + (l - abs(m)) * C, 16), lanes]
                 for j in range(2 * l + 1):
                     total = None
                     for m in range(-within, within + 1):
@@ -196,81 +197,78 @@
     def chunk_cols(q):
         return pl.ds(CHUNKS[q][1] * C, CHUNKS[q][2] * C)
 
-    def back(q, part, axis, where):
+    def back(q, part, i, axis, where):
         cols = chunk_cols(q)
-        side = 0 if where is down else 1
-        k = q * 6 + part * 2 + side
         src, dst = ((sp, ry), (sz, rz), (st, rt))[part]
-        index = (side, slice(None), slice(None), cols) if part == 0 else (side, slice(None), cols)
-        return remote(src.at[index], dst.at[index], bs.at[k], br.at[k], axis, where)
-
+        k = q * 10 + part * 4 + i
+        return remote(
+            src.at[i, :, cols], dst.at[i, :, cols], bs.at[k], br.at[k], axis, where
+        )
+
+    routes = (
+        (("gy", down), ("gz", up), ("gz", down), ("gy", up)),
+        (("gy", down), ("gz", down), ("gz", up), ("gy", up)),
+        (("gx", down), ("gx", up)),
+    )
     backs = [
-        [[back(q, part, axis, where) for where in (down, up)]
-         for part, axis in enumerate(("gy", "gz", "gx"))]
+        [[back(q, part, i, *route) for i, route in enumerate(routes[part])] for part in range(3)]
         for q in range(NCH)
     ]
 
     def along(q):
         cols = chunk_cols(q)
-        for copy in backs[q][0]:
-            copy.wait_recv()
-        for f in (0, 2):
-            total = sc[f, :, cols] + ry[0, f, :, cols].astype(F32) + ry[1, f, :, cols].astype(F32)
-            sz[f // 2, :, cols] = total.astype(BF16)
-        for copy in backs[q][1]:
-            copy.start()
-        acc[:, cols] = sc[1, :, cols] + ry[0, 1, :, cols].astype(F32) + ry[1, 1, :, cols].astype(F32)
-
+        for side, corner in ((1, 0), (0, 1), (3, 2), (2, 3)):
+            backs[q][0][corner].wait_recv()
+            sz[side, :, cols] = (sc[side, :, cols] + ry[corner, :, cols].astype(F32)).astype(BF16)
+            backs[q][1][side].start()
+
+    first[3].wait_recv()
+    relays[2].start()
+    first[2].wait_recv()
+    relays[3].start()
+
+    first[4].wait_recv()
+    first[5].wait_recv()
+    lax.fori_loop(0, COEFS, gather_tower, 0, unroll=True)
     first[0].wait_recv()
     relays[0].start()
+    first[1].wait_recv()
     relays[1].start()
-    first[1].wait_recv()
-    relays[2].start()
-    relays[3].start()
-
-    first[4].wait_recv()
-    first[5].wait_recv()
-    lax.fori_loop(0, COEFS, gather_tower, 0, unroll=5)
     lax.fori_loop(0, 8, rotate, 0)
     mix()
     for q, (degrees, low, many) in enumerate(CHUNKS):
         rotate_back(degrees)
 
-        def scatter_plate(i, c):
+        for i in range(low, low + many):
             s = lax.dot_general(pick_p[...], msg[i], NT, preferred_element_type=F32)
-            col = column(i)
-            for f in range(3):
-                sp[0, f, :, col] = s[f * A : (f + 1) * A].astype(BF16)
-                sc[f, :, col] = s[(3 + f) * A : (4 + f) * A]
-                sp[1, f, :, col] = s[(6 + f) * A : (7 + f) * A].astype(BF16)
-            return c
-
-        lax.fori_loop(low, low + many, scatter_plate, 0)
+            col = pl.ds(i * C, C)
+            for k, p in enumerate((0, 2, 6, 8)):
+                sp[k, :, col] = s[p * A : (p + 1) * A].astype(BF16)
+            for k, p in enumerate((1, 3, 5, 7, 4)):
+                sc[k, :, col] = s[p * A : (p + 1) * A]
         for copy in backs[q][0]:
             copy.start()
 
-    for copy in first[2:4] + relays:
+    for copy in relays:
         copy.wait_recv()
-    lax.fori_loop(0, COEFS, gather_plate, 0, unroll=5)
+    lax.fori_loop(0, COEFS, gather_plate, 0, unroll=True)
     lax.fori_loop(0, 8, rotate, 0)
     along(0)
     mix()
     along(1)
-    along(2)
     for q, (degrees, low, many) in enumerate(CHUNKS):
         rotate_back(degrees)
 
-        def scatter_tower(i, c):
+        for i in range(low, low + many):
             s = lax.dot_general(pick_t[...], msg[i], NT, preferred_element_type=F32)
-            col = column(i)
+            col = pl.ds(i * C, C)
             st[0, :, col] = s[0:A].astype(BF16)
             tc[:, col] = s[A : 2 * A]
             st[1, :, col] = s[2 * A : 3 * A].astype(BF16)
-            return c
-
-        lax.fori_loop(low, low + many, scatter_tower, 0)
         for copy in backs[q][2]:
             copy.start()
+        if q == 0:
+            along(2)
 
     present = lax.broadcasted_iota(jnp.int32, (A, C), 0) < atoms_s[0, 0]
     for q, (degrees, low, many) in enumerate(CHUNKS):
@@ -281,7 +279,8 @@
             col = column(i)
             total = (
                 tc[:, col] + rt[0, :, col].astype(F32) + rt[1, :, col].astype(F32)
-                + acc[:, col] + rz[0, :, col].astype(F32) + rz[1, :, col].astype(F32)
+                + sc[4, :, col] + rz[0, :, col].astype(F32) + rz[1, :, col].astype(F32)
+                + rz[2, :, col].astype(F32) + rz[3, :, col].astype(F32)
                 + x[OWN, :, col].astype(F32)
             )
             out[:, col] = jnp.where(present, total, 0.0).astype(BF16)
@@ -312,14 +311,16 @@
             V((ROWS, 8, E), F32), V((C, E), F32),
             V((640, 640), BF16), V((512, 1024), BF16), V((384, 768), BF16),
             V((3 * A, E), BF16), V((9 * A, E), BF16),
-            V((COEFS, C, E), F32), V((640, E), BF16), V((1536, E), BF16), V((1152, E), BF16),
-            V((640, E), F32), V((2, 512, E), F32), V((2, 384, E), F32), V((COEFS, C, E), BF16),
-            V((2, 3, A, F), BF16), V((3, A, F), F32), V((2, 3, A, F), BF16),
-            V((2, A, F), BF16), V((2, A, F), BF16), V((A, F), F32),
+            V((COEFS, C, E), F32), V((640, E), BF16), V((1024, 2 * E), BF16), V((768, 2 * E), BF16),
+            V((640, E), F32), V((512, 2 * E), F32), V((384, 2 * E), F32), V((COEFS, C, E), BF16),
+            V((4, A, F), BF16), V((5, A, F), F32), V((4, A, F), BF16),
+            V((4, A, F), BF16), V((4, A, F), BF16),
             V((2, A, F), BF16), V((A, F), F32), V((2, A, F), BF16),
-            pltpu.SMEM((1, 1), jnp.int32), pltpu.SMEM((1, 1), jnp.int32), dma((10,)), dma((10,)), dma((10,)), dma((6 * NCH,)), dma((6 * NCH,)),
+            pltpu.SMEM((1, 1), jnp.int32), pltpu.SMEM((1, 1), jnp.int32), dma((10,)), dma((10,)), dma((10,)), dma((10 * NCH,)), dma((10 * NCH,)),
         ],
-        compiler_params=pltpu.CompilerParams(collective_id=0, has_side_effects=True),
+        compiler_params=pltpu.CompilerParams(
+            collective_id=0, has_side_effects=True
+        ),
         name="layer",
     )(
         features.reshape(A, F), box_atoms.reshape(1, 1), edge_count.reshape(1, 1),

time: 47.2 us -> 40.8 us (0.86)
  Pallas kernels: 44.2 us -> 37.7 us
    pallas_call x1, Pallas kernels: 44.2 us -> 37.7 us  [body(): pl.pallas_call(kernel, out_shape=jax.ShapeDtypeStruct((A, F), BF16), in_s...]
where the time goes in v2:
time: 40.8 us; the launch traced here: 40.6 us
  Pallas kernels  37.7 us (92%)
  local copies, waits for them, and re-layouts  1.54 us (4%)
  between operations  1.3 us (3%)
    pallas_call x1, Pallas kernels, body(): pl.pallas_call(kernel, out_shape=jax.ShapeDtypeStruct((A, F), BF16), in_s...  37.7 us
    unnamed x1, local copies, waits for them, and re-layouts  1.54 us

profile of v2, /device:TPU:1, one launch (start us, length us, event | category | flops | bytes accessed | tf_op | source)
XLA Modules:
  0.0 40.6 jit_solution(3352070013073734679)
XLA Ops:
  1.3 37.7 %layer.1 = bf16[16,3200]{1,0:T(8,128)(2,1)} custom-call(bf16[16,3200]{1,0:T(8,128)(2,1)} %bitcast.12, s32[1,1]{1,0:T(1,128)} %bitcast.8.atoms_h, s32[1,1]{1,0:T(1,128)} %bitcast.9.count_h, s32[1,256]{1,0:T(1,128)} %bitcast.14, s32[1,256]{1,0:T(1,128)} %bitcast.15, f32[115,1,256]{2,1,0:T(1,128)} %bitcast.11, bf16[256,128]{1,0:T(8,128)(2,1)} %bitcast.13, ...), custom_call_target="tpu_custom_call" | custom-call | tf_op jit(solution)/shard_map/layer/pallas_call | solution.py:303
  39.0 1.5 %copy.14 = bf16[1,1,1,16,3200]{4,3,2,1,0:T(8,128)(2,1)} copy(bf16[1,1,1,16,3200]{4,3,2,1,0:T(8,128)(2,1)} %bitcast.10) | data formatting | bytes 204800

commit v3 on v2

--- a/solution.py
+++ b/solution.py
@@ -27,6 +27,7 @@
 
 CHUNKS = (((4,), 16, 9), ((3,), 9, 7), ((0, 1, 2), 0, 9))
 NCH = len(CHUNKS)
+HALVES = ((0, 13 * C), (13 * C, 12 * C))
 OWN = 4
 XLOW, XHIGH = 9, 10
 
@@ -75,20 +76,35 @@
     loads[0].wait()
     pl.semaphore_wait(barrier, 6)
 
-    def forward(k, src, dst, axis, where):
-        return remote(x.at[src], x.at[dst], fs.at[k], fr.at[k], axis, where)
+    def forward(k, src, dst, axis, where, half=None):
+        if half is None:
+            return remote(x.at[src], x.at[dst], fs.at[k], fr.at[k], axis, where)
+        cols = pl.ds(*HALVES[half])
+        k = k + 10 * half
+        return remote(x.at[src, :, cols], x.at[dst, :, cols], fs.at[k], fr.at[k], axis, where)
 
     first = [
-        forward(0, OWN, 3, "gz", up), forward(1, OWN, 5, "gz", down),
-        forward(2, OWN, 1, "gy", up), forward(3, OWN, 7, "gy", down),
-        forward(4, OWN, XLOW, "gx", up), forward(5, OWN, XHIGH, "gx", down),
+        [
+            forward(0, OWN, 3, "gz", up, h), forward(1, OWN, 5, "gz", down, h),
+            forward(2, OWN, 1, "gy", up, h), forward(3, OWN, 7, "gy", down, h),
+        ]
+        for h in range(2)
     ]
+    towers = [forward(4, OWN, XLOW, "gx", up), forward(5, OWN, XHIGH, "gx", down)]
     relays = [
-        forward(6, 3, 0, "gy", up), forward(7, 5, 8, "gy", down),
-        forward(8, 7, 6, "gz", up), forward(9, 1, 2, "gz", down),
+        [
+            forward(6, 3, 0, "gy", up, h), forward(7, 5, 8, "gy", down, h),
+            forward(9, 1, 2, "gz", down, h), forward(8, 7, 6, "gz", up, h),
+        ]
+        for h in range(2)
     ]
-    for copy in first:
+    for copy in towers + first[0] + first[1]:
         copy.start()
+
+    def pass_on(half):
+        for i in (2, 3, 0, 1):
+            first[half][i].wait_recv()
+            relays[half][i].start()
 
     for load in loads[1:]:
         load.wait()
@@ -110,17 +126,20 @@
         return pl.ds(pl.multiple_of(i * C, C), C)
 
     def turn0(i, c):
-        w0t[column(i), :] = w0[:, column(i)].T
+        for k in range(5):
+            w0t[k, column(i), :] = w0[k * C : (k + 1) * C, column(i)].T
         return c
 
     def turn1(i, c):
-        w1t[column(i), 0:512] = w1[1, :, column(i)].T
-        w1t[column(i), 512:1024] = w1[0, :, column(i)].T
+        for k in range(4):
+            w1t[k, column(i), :] = w1[1, k * C : (k + 1) * C, column(i)].T
+            w1t[4 + k, column(i), :] = w1[0, k * C : (k + 1) * C, column(i)].T
         return c
 
     def turn2(i, c):
-        w2t[column(i), 0:384] = w2[1, :, column(i)].T
-        w2t[column(i), 384:768] = w2[0, :, column(i)].T
+        for k in range(3):
+            w2t[k, column(i), :] = w2[1, k * C : (k + 1) * C, column(i)].T
+            w2t[3 + k, column(i), :] = w2[0, k * C : (k + 1) * C, column(i)].T
         return c
 
     lax.fori_loop(0, 5, turn0, 0)
@@ -167,9 +186,9 @@
         return c
 
     def mix():
-        y0[...] = jnp.dot(w0t[...], l0[...], preferred_element_type=F32)
-        y1[...] = jnp.dot(w1t[...], l1[...], preferred_element_type=F32)
-        y2[...] = jnp.dot(w2t[...], l2[...], preferred_element_type=F32)
+        for y, w, low in ((y0, w0t, l0), (y1, w1t, l1), (y2, w2t, l2)):
+            table = jnp.concatenate([w[k] for k in range(w.shape[0])], axis=1)
+            y[...] = jnp.dot(table, low[...], preferred_element_type=F32)
 
     def rotate_back(degrees):
         def step(t, c):
@@ -222,18 +241,11 @@
             sz[side, :, cols] = (sc[side, :, cols] + ry[corner, :, cols].astype(F32)).astype(BF16)
             backs[q][1][side].start()
 
-    first[3].wait_recv()
-    relays[2].start()
-    first[2].wait_recv()
-    relays[3].start()
-
-    first[4].wait_recv()
-    first[5].wait_recv()
+    pass_on(0)
+    for copy in towers:
+        copy.wait_recv()
     lax.fori_loop(0, COEFS, gather_tower, 0, unroll=True)
-    first[0].wait_recv()
-    relays[0].start()
-    first[1].wait_recv()
-    relays[1].start()
+    pass_on(1)
     lax.fori_loop(0, 8, rotate, 0)
     mix()
     for q, (degrees, low, many) in enumerate(CHUNKS):
@@ -249,7 +261,7 @@
         for copy in backs[q][0]:
             copy.start()
 
-    for copy in relays:
+    for copy in relays[0] + relays[1]:
         copy.wait_recv()
     lax.fori_loop(0, COEFS, gather_plate, 0, unroll=True)
     lax.fori_loop(0, 8, rotate, 0)
@@ -270,24 +282,18 @@
         if q == 0:
             along(2)
 
-    present = lax.broadcasted_iota(jnp.int32, (A, C), 0) < atoms_s[0, 0]
-    for q, (degrees, low, many) in enumerate(CHUNKS):
+    for q in range(NCH):
         for copy in backs[q][1] + backs[q][2]:
             copy.wait_recv()
 
-        def finish(i, c):
-            col = column(i)
-            total = (
-                tc[:, col] + rt[0, :, col].astype(F32) + rt[1, :, col].astype(F32)
-                + sc[4, :, col] + rz[0, :, col].astype(F32) + rz[1, :, col].astype(F32)
-                + rz[2, :, col].astype(F32) + rz[3, :, col].astype(F32)
-                + x[OWN, :, col].astype(F32)
-            )
-            out[:, col] = jnp.where(present, total, 0.0).astype(BF16)
-            return c
-
-        lax.fori_loop(low, low + many, finish, 0)
-    for copy in first + relays:
+        cols = chunk_cols(q)
+        present = lax.broadcasted_iota(jnp.int32, (A, CHUNKS[q][2] * C), 0) < atoms_s[0, 0]
+        total = tc[:, cols] + sc[4, :, cols] + x[OWN, :, cols].astype(F32)
+        for ref, parts in ((rt, 2), (rz, 4)):
+            for i in range(parts):
+                total = total + ref[i, :, cols].astype(F32)
+        out[:, cols] = jnp.where(present, total, 0.0).astype(BF16)
+    for copy in first[0] + first[1] + towers + relays[0] + relays[1]:
         copy.wait_send()
     for q in range(NCH):
         for part in backs[q]:
@@ -309,14 +315,14 @@
             V((11, A, F), BF16), V((1, E), jnp.int32), V((1, E), jnp.int32), V((ROWS, 1, E), F32),
             V((E, C), BF16), V((640, 640), BF16), V((2, 512, 512), BF16), V((2, 384, 384), BF16),
             V((ROWS, 8, E), F32), V((C, E), F32),
-            V((640, 640), BF16), V((512, 1024), BF16), V((384, 768), BF16),
+            V((5, 640, C), BF16), V((8, 512, C), BF16), V((6, 384, C), BF16),
             V((3 * A, E), BF16), V((9 * A, E), BF16),
             V((COEFS, C, E), F32), V((640, E), BF16), V((1024, 2 * E), BF16), V((768, 2 * E), BF16),
             V((640, E), F32), V((512, 2 * E), F32), V((384, 2 * E), F32), V((COEFS, C, E), BF16),
             V((4, A, F), BF16), V((5, A, F), F32), V((4, A, F), BF16),
             V((4, A, F), BF16), V((4, A, F), BF16),
             V((2, A, F), BF16), V((A, F), F32), V((2, A, F), BF16),
-            pltpu.SMEM((1, 1), jnp.int32), pltpu.SMEM((1, 1), jnp.int32), dma((10,)), dma((10,)), dma((10,)), dma((10 * NCH,)), dma((10 * NCH,)),
+            pltpu.SMEM((1, 1), jnp.int32), pltpu.SMEM((1, 1), jnp.int32), dma((10,)), dma((20,)), dma((20,)), dma((10 * NCH,)), dma((10 * NCH,)),
         ],
         compiler_params=pltpu.CompilerParams(
             collective_id=0, has_side_effects=True

time: 40.8 us -> 39.8 us (0.975)
  Pallas kernels: 37.7 us -> 36.8 us
    pallas_call x1, Pallas kernels: 37.7 us -> 36.8 us  [body(): pl.pallas_call(kernel, out_shape=jax.ShapeDtypeStruct((A, F), BF16), in_s...]
where the time goes in v3:
time: 39.8 us; the launch traced here: 39.7 us
  Pallas kernels  36.8 us (92%)
  local copies, waits for them, and re-layouts  1.54 us (4%)
  between operations  1.3 us (3%)
    pallas_call x1, Pallas kernels, body(): pl.pallas_call(kernel, out_shape=jax.ShapeDtypeStruct((A, F), BF16), in_s...  36.8 us
    unnamed x1, local copies, waits for them, and re-layouts  1.54 us

profile of v3, /device:TPU:1, one launch (start us, length us, event | category | flops | bytes accessed | tf_op | source)
XLA Modules:
  0.0 39.7 jit_solution(11108622502812847761)
XLA Ops:
  1.3 36.8 %layer.1 = bf16[16,3200]{1,0:T(8,128)(2,1)} custom-call(bf16[16,3200]{1,0:T(8,128)(2,1)} %bitcast.12, s32[1,1]{1,0:T(1,128)} %bitcast.8.atoms_h, s32[1,1]{1,0:T(1,128)} %bitcast.9.count_h, s32[1,256]{1,0:T(1,128)} %bitcast.14, s32[1,256]{1,0:T(1,128)} %bitcast.15, f32[115,1,256]{2,1,0:T(1,128)} %bitcast.11, bf16[256,128]{1,0:T(8,128)(2,1)} %bitcast.13, ...), custom_call_target="tpu_custom_call" | custom-call | tf_op jit(solution)/shard_map/layer/pallas_call | solution.py:309
  38.1 1.5 %copy.14 = bf16[1,1,1,16,3200]{4,3,2,1,0:T(8,128)(2,1)} copy(bf16[1,1,1,16,3200]{4,3,2,1,0:T(8,128)(2,1)} %bitcast.10) | data formatting | bytes 204800

commit v4 on v3

--- a/solution.py
+++ b/solution.py
@@ -109,8 +109,8 @@
     for load in loads[1:]:
         load.wait()
     for o in range(ROWS):
-        wb[o] = jnp.broadcast_to(wig[o], (8, wig.shape[2]))
-    gate[...] = rad[...].T.astype(F32)
+        wb[o] = jnp.broadcast_to(wig[o].astype(BF16), (16, wig.shape[2]))
+    gate[...] = rad[...].T
     live = lax.broadcasted_iota(jnp.int32, et.shape, 1) < count_s[0, 0]
     edges = et.shape[1]
     here_t = jnp.where(live, et[...], -1)
@@ -147,18 +147,23 @@
     lax.fori_loop(0, 3, turn2, 0)
 
     def spread(o):
-        row = wb[o]
-        return jnp.concatenate([row, row], axis=0)
+        return wb[o]
+
+    def added(terms):
+        while len(terms) > 1:
+            pairs = [a + b for a, b in zip(terms[::2], terms[1::2])]
+            terms = pairs + terms[len(terms) - len(terms) % 2 :]
+        return terms[0]
 
     def gather_tower(i, c):
         col = column(i)
         block = jnp.concatenate([x[XLOW, :, col], x[OWN, :, col], x[XHIGH, :, col]], axis=0)
-        g[i] = lax.dot_general(block, pick_t[...], TN, preferred_element_type=F32)
+        g[i] = lax.dot_general(block, pick_t[...], TN, preferred_element_type=F32).astype(BF16)
         return c
 
     def gather_plate(i, c):
         block = x[0:9, :, column(i)].reshape(9 * A, C)
-        g[i] = lax.dot_general(block, pick_p[...], TN, preferred_element_type=F32)
+        g[i] = lax.dot_general(block, pick_p[...], TN, preferred_element_type=F32).astype(BF16)
         return c
 
     def rotate(t, c):
@@ -168,10 +173,7 @@
         for l in range(DEGREE + 1):
             xs = [g[l * l + j, tile, :] for j in range(2 * l + 1)]
             for m in range(-min(l, ORDER), min(l, ORDER) + 1):
-                total = spread(WIG[l, m]) * xs[0]
-                for j in range(1, 2 * l + 1):
-                    total = total + spread(WIG[l, m] + j) * xs[j]
-                low = (total * scale).astype(BF16)
+                low = added([spread(WIG[l, m] + j) * xs[j] for j in range(2 * l + 1)]) * scale
                 if m == 0:
                     l0[pl.ds(base + l * C, 16), :] = low
                 else:
@@ -188,7 +190,7 @@
     def mix():
         for y, w, low in ((y0, w0t, l0), (y1, w1t, l1), (y2, w2t, l2)):
             table = jnp.concatenate([w[k] for k in range(w.shape[0])], axis=1)
-            y[...] = jnp.dot(table, low[...], preferred_element_type=F32)
+            y[...] = jnp.dot(table, low[...], preferred_element_type=F32).astype(BF16)
 
     def rotate_back(degrees):
         def step(t, c):
@@ -204,11 +206,9 @@
                         lanes = slice(0, E) if m > 0 else slice(E, 2 * E)
                         ys[m] = ref[pl.ds(base + (l - abs(m)) * C, 16), lanes]
                 for j in range(2 * l + 1):
-                    total = None
-                    for m in range(-within, within + 1):
-                        term = spread(WIG[l, m] + j) * ys[m]
-                        total = term if total is None else total + term
-                    msg[l * l + j, pl.ds(base, 16), :] = total.astype(BF16)
+                    msg[l * l + j, pl.ds(base, 16), :] = added(
+                        [spread(WIG[l, m] + j) * ys[m] for m in range(-within, within + 1)]
+                    )
             return c
 
         lax.fori_loop(0, 8, step, 0)
@@ -314,11 +314,11 @@
         scratch_shapes=[
             V((11, A, F), BF16), V((1, E), jnp.int32), V((1, E), jnp.int32), V((ROWS, 1, E), F32),
             V((E, C), BF16), V((640, 640), BF16), V((2, 512, 512), BF16), V((2, 384, 384), BF16),
-            V((ROWS, 8, E), F32), V((C, E), F32),
+            V((ROWS, 16, E), BF16), V((C, E), BF16),
             V((5, 640, C), BF16), V((8, 512, C), BF16), V((6, 384, C), BF16),
             V((3 * A, E), BF16), V((9 * A, E), BF16),
-            V((COEFS, C, E), F32), V((640, E), BF16), V((1024, 2 * E), BF16), V((768, 2 * E), BF16),
-            V((640, E), F32), V((512, 2 * E), F32), V((384, 2 * E), F32), V((COEFS, C, E), BF16),
+            V((COEFS, C, E), BF16), V((640, E), BF16), V((1024, 2 * E), BF16), V((768, 2 * E), BF16),
+            V((640, E), BF16), V((512, 2 * E), BF16), V((384, 2 * E), BF16), V((COEFS, C, E), BF16),
             V((4, A, F), BF16), V((5, A, F), F32), V((4, A, F), BF16),
             V((4, A, F), BF16), V((4, A, F), BF16),
             V((2, A, F), BF16), V((A, F), F32), V((2, A, F), BF16),

time: 39.8 us -> 38.9 us (0.977)
  Pallas kernels: 36.8 us -> 35.9 us
    pallas_call x1, Pallas kernels: 36.8 us -> 35.9 us  [body(): pl.pallas_call(kernel, out_shape=jax.ShapeDtypeStruct((A, F), BF16), in_s...]
where the time goes in v4:
time: 38.9 us; the launch traced here: 38.8 us
  Pallas kernels  35.9 us (92%)
  local copies, waits for them, and re-layouts  1.54 us (4%)
  between operations  1.3 us (3%)
    pallas_call x1, Pallas kernels, body(): pl.pallas_call(kernel, out_shape=jax.ShapeDtypeStruct((A, F), BF16), in_s...  35.9 us
    unnamed x1, local copies, waits for them, and re-layouts  1.54 us

profile of v4, /device:TPU:1, one launch (start us, length us, event | category | flops | bytes accessed | tf_op | source)
XLA Modules:
  0.0 38.8 jit_solution(1158987683788652251)
XLA Ops:
  1.3 35.9 %layer.1 = bf16[16,3200]{1,0:T(8,128)(2,1)} custom-call(bf16[16,3200]{1,0:T(8,128)(2,1)} %bitcast.12, s32[1,1]{1,0:T(1,128)} %bitcast.8.atoms_h, s32[1,1]{1,0:T(1,128)} %bitcast.9.count_h, s32[1,256]{1,0:T(1,128)} %bitcast.14, s32[1,256]{1,0:T(1,128)} %bitcast.15, f32[115,1,256]{2,1,0:T(1,128)} %bitcast.11, bf16[256,128]{1,0:T(8,128)(2,1)} %bitcast.13, ...), custom_call_target="tpu_custom_call" | custom-call | tf_op jit(solution)/shard_map/layer/pallas_call | solution.py:309
  37.2 1.5 %copy.14 = bf16[1,1,1,16,3200]{4,3,2,1,0:T(8,128)(2,1)} copy(bf16[1,1,1,16,3200]{4,3,2,1,0:T(8,128)(2,1)} %bitcast.10) | data formatting | bytes 204800

commit v5 on v4

--- a/solution.py
+++ b/solution.py
@@ -35,7 +35,7 @@
 def kernel(
     feat_h, atoms_h, count_h, et_h, ep_h, wig_h, rad_h, w0_h, w1_h, w2_h,
     out,
-    x, et, ep, wig, rad, w0, w1, w2, wb, gate, w0t, w1t, w2t, pick_t, pick_p,
+    x, et, ep, wig, rad, w0, w1, w2, wb, wf, gate, w0t, w1t, w2t, pick_t, pick_p,
     g, l0, l1, l2, y0, y1, y2, msg,
     sp, sc, ry, sz, rz, st, tc, rt,
     atoms_s, count_s, local, fs, fr, bs, br,
@@ -109,6 +109,7 @@
     for load in loads[1:]:
         load.wait()
     for o in range(ROWS):
+        wf[o] = jnp.broadcast_to(wig[o], (8, wig.shape[2]))
         wb[o] = jnp.broadcast_to(wig[o].astype(BF16), (16, wig.shape[2]))
     gate[...] = rad[...].T
     live = lax.broadcasted_iota(jnp.int32, et.shape, 1) < count_s[0, 0]
@@ -148,6 +149,10 @@
 
     def spread(o):
         return wb[o]
+
+    def spread_full(o):
+        row = wf[o]
+        return jnp.concatenate([row, row], axis=0)
 
     def added(terms):
         while len(terms) > 1:
@@ -190,7 +195,7 @@
     def mix():
         for y, w, low in ((y0, w0t, l0), (y1, w1t, l1), (y2, w2t, l2)):
             table = jnp.concatenate([w[k] for k in range(w.shape[0])], axis=1)
-            y[...] = jnp.dot(table, low[...], preferred_element_type=F32).astype(BF16)
+            y[...] = jnp.dot(table, low[...], preferred_element_type=F32)
 
     def rotate_back(degrees):
         def step(t, c):
@@ -207,8 +212,8 @@
                         ys[m] = ref[pl.ds(base + (l - abs(m)) * C, 16), lanes]
                 for j in range(2 * l + 1):
                     msg[l * l + j, pl.ds(base, 16), :] = added(
-                        [spread(WIG[l, m] + j) * ys[m] for m in range(-within, within + 1)]
-                    )
+                        [spread_full(WIG[l, m] + j) * ys[m] for m in range(-within, within + 1)]
+                    ).astype(BF16)
             return c
 
         lax.fori_loop(0, 8, step, 0)
@@ -314,11 +319,11 @@
         scratch_shapes=[
             V((11, A, F), BF16), V((1, E), jnp.int32), V((1, E), jnp.int32), V((ROWS, 1, E), F32),
             V((E, C), BF16), V((640, 640), BF16), V((2, 512, 512), BF16), V((2, 384, 384), BF16),
-            V((ROWS, 16, E), BF16), V((C, E), BF16),
+            V((ROWS, 16, E), BF16), V((ROWS, 8, E), F32), V((C, E), BF16),
             V((5, 640, C), BF16), V((8, 512, C), BF16), V((6, 384, C), BF16),
             V((3 * A, E), BF16), V((9 * A, E), BF16),
             V((COEFS, C, E), BF16), V((640, E), BF16), V((1024, 2 * E), BF16), V((768, 2 * E), BF16),
-            V((640, E), BF16), V((512, 2 * E), BF16), V((384, 2 * E), BF16), V((COEFS, C, E), BF16),
+            V((640, E), F32), V((512, 2 * E), F32), V((384, 2 * E), F32), V((COEFS, C, E), BF16),
             V((4, A, F), BF16), V((5, A, F), F32), V((4, A, F), BF16),
             V((4, A, F), BF16), V((4, A, F), BF16),
             V((2, A, F), BF16), V((A, F), F32), V((2, A, F), BF16),

time: 38.9 us -> 39.2 us (level)
  no operation moved by 1% of the time
where the time goes in v5:
time: 39.2 us; the launch traced here: 39.1 us
  Pallas kernels  36.2 us (92%)
  local copies, waits for them, and re-layouts  1.54 us (4%)
  between operations  1.3 us (3%)
    pallas_call x1, Pallas kernels, body(): pl.pallas_call(kernel, out_shape=jax.ShapeDtypeStruct((A, F), BF16), in_s...  36.2 us
    unnamed x1, local copies, waits for them, and re-layouts  1.54 us

profile of v5, /device:TPU:1, one launch (start us, length us, event | category | flops | bytes accessed | tf_op | source)
XLA Modules:
  0.0 39.1 jit_solution(10719048250618984060)
XLA Ops:
  1.3 36.2 %layer.1 = bf16[16,3200]{1,0:T(8,128)(2,1)} custom-call(bf16[16,3200]{1,0:T(8,128)(2,1)} %bitcast.12, s32[1,1]{1,0:T(1,128)} %bitcast.8.atoms_h, s32[1,1]{1,0:T(1,128)} %bitcast.9.count_h, s32[1,256]{1,0:T(1,128)} %bitcast.14, s32[1,256]{1,0:T(1,128)} %bitcast.15, f32[115,1,256]{2,1,0:T(1,128)} %bitcast.11, bf16[256,128]{1,0:T(8,128)(2,1)} %bitcast.13, ...), custom_call_target="tpu_custom_call" | custom-call | tf_op jit(solution)/shard_map/layer/pallas_call | solution.py:314
  37.5 1.5 %copy.14 = bf16[1,1,1,16,3200]{4,3,2,1,0:T(8,128)(2,1)} copy(bf16[1,1,1,16,3200]{4,3,2,1,0:T(8,128)(2,1)} %bitcast.10) | data formatting | bytes 204800
